TPU v7x, 32 devices: a whole 2x2x4 slice. The times are simulated.
32 devices in a mesh: dp: 4 (over x, y), tp: 8 (over z, core).
Axes of the slice: x: 2, y: 2, z: 4, core: 2. Of those that a mesh axis runs over, the one named last changes fastest.
Arguments:
- x: bfloat16 [8192, 8192], P('dp'), parts along dimension 0
- w_gate: bfloat16 [8192, 24576], P(None, 'tp')
- w_up: bfloat16 [8192, 24576], P(None, 'tp')
- w_down: bfloat16 [24576, 8192], P('tp')
Outputs:
- output: bfloat16 [8192, 8192], P('dp'), parts along dimension 0
There are 4 independent parts. A program takes and returns all parts, laid end to end along the dimension named above; an argument that names none is the same for every part.
All inputs are finite; a program needn't handle non-finite values.
Results may differ from a plain program's by a relative error of at most 0.016.
Values are sent between devices in bfloat16 or wider.
A program may use at most 2 GiB of HBM per device.

v0:
```python
import jax
import jax.numpy as jnp
from jax import lax
from jax.sharding import PartitionSpec as P


def solution(mesh):
    def step(x, w_gate, w_up, w_down):
        gate = jnp.dot(x, w_gate, preferred_element_type=jnp.float32)
        up = jnp.dot(x, w_up, preferred_element_type=jnp.float32)
        hidden = (jax.nn.silu(gate) * up).astype(jnp.bfloat16)
        term = jnp.dot(hidden, w_down, preferred_element_type=jnp.float32).astype(jnp.bfloat16)
        return lax.psum(term, "tp")

    return jax.shard_map(
        step,
        mesh=mesh,
        in_specs=(P("dp", None), P(None, "tp"), P(None, "tp"), P("tp", None)),
        out_specs=P("dp", None),
        check_vma=False,
    )
```

profile of v0, /device:TPU:0, one launch (start us, length us, event | category | flops | bytes accessed | tf_op | source)
XLA Modules:
  0.0 1039.9 jit_solution(14837353237011795365)
XLA Ops:
  6.5 0.0 all-reduce.2.cloned.1.call-start
  6.5 116.1 %fusion = f32[2048,3072]{1,0:T(8,128)} fusion(bf16[2048,8192]{1,0:T(8,128)(2,1)} %param.4, bf16[8192,3072]{1,0:T(8,128)(2,1)} %param.5), kind=kOutput, calls=%fused_computation.2 | convolution fusion | flops 103079215104 | bytes 109051904 | tf_op jit(solution)/shard_map/dot_general | solution.py:9
  122.7 121.7 %multiply_convert_fusion = bf16[2048,3072]{1,0:T(8,128)(2,1)} fusion(f32[2048,3072]{1,0:T(8,128)} %fusion, bf16[2048,8192]{1,0:T(8,128)(2,1)} %param.4, bf16[8192,3072]{1,0:T(8,128)(2,1)} %param.6), kind=kOutput, calls=%fused_computation.1 | convolution fusion | flops 103116963840 | bytes 121634816 | tf_op jit(solution)/shard_map/dot_general | solution.py:10
  244.3 114.5 %convolution_convert_fusion = bf16[2048,8192]{1,0:T(8,128)(2,1)} fusion(bf16[2048,3072]{1,0:T(8,128)(2,1)} %multiply_convert_fusion, bf16[3072,8192]{1,0:T(8,128)(2,1)} %param.7), kind=kOutput, calls=%fused_computation | convolution fusion | flops 103095992320 | bytes 96468992 | tf_op jit(solution)/shard_map/dot_general | solution.py:12
  358.9 0.0 all-reduce.2.cloned.1.call-update
  358.9 651.2 %all-reduce.2.cloned.1.call-done = bf16[2048,8192]{1,0:T(8,128)(2,1)} async-done(((bf16[2048,8192]{1,0:T(8,128)(2,1)}), bf16[2048,8192]{1,0:T(8,128)(2,1)}) %all-reduce.2.cloned.1.call-update) | async-done | bytes 33554448 | tf_op jit(solution)/shard_map/psum | solution.py:13
  1010.1 23.0 %copy.6 = bf16[2048,8192]{1,0:T(8,128)(2,1)} copy(bf16[2048,8192]{1,0:T(8,128)(2,1)} %all-reduce.2.cloned.1.call-done) | data formatting | bytes 67108864
Async XLA Ops:
  6.5 1003.6 %all-reduce.2.cloned.1.call-start = ((), (), s32[]{:S(2)}) async-start(), calls=%async_computation | async-start | bytes 67108864 | tf_op jit(solution)/shard_map/psum | solution.py:13
Sparse Core Ops, SparseCore 0:
  359.0 651.0 all-reduce.1
where the time goes:
time: 1040 us
  waiting for transfers between devices  651 us (63%)
  matrix products  352 us (34%)
  local copies, waits for them, and re-layouts  23 us (2%)
  between operations  13.4 us (1%)
    psum x1, waiting for transfers between devices, step(): return lax.psum(term, 'tp')  651 us
    dot_general x1, matrix products, step(): up = jnp.dot(x, w_up, preferred_element_type=jnp.float32)  122 us
    dot_general x1, matrix products, step(): gate = jnp.dot(x, w_gate, preferred_element_type=jnp.float32)  116 us
    dot_general x1, matrix products, step(): jnp.dot(hidden, w_down, preferred_element_type=jnp.float32)  115 us
    unnamed x1, local copies, waits for them, and re-layouts  23 us
  transfers between devices with their start and end apart: 1, of which 1 were waited for; matrix products, arithmetic and copies ran while one was open for 0% of the time, Pallas kernels for 0%

commit v1 on v0

v1 whole, which is shorter than its diff:
```python
import functools

import jax
import jax.numpy as jnp
from jax import lax
from jax.experimental import pallas as pl
from jax.experimental.pallas import tpu as pltpu
from jax.sharding import PartitionSpec as P

MESH = pl.DeviceIdType.MESH
BF16, F32 = jnp.bfloat16, jnp.float32
BLOCK, CHUNK, NA = 512, 128, 256
VMEM = 67043328
LAGS = (1, 3, 5, 7)


def kernel(
    x, wg, wu, wd,
    y, cin, xin,
    xb, hb, wa, wb, part, sent, psend, pbuf, cload, xload, xsend, tsend,
    sx, sa, sb, p_send, p_recv, p_free, o_send, c_recv, x_send, x_recv,
    t_send, y_recv, f_send, g_send, yp_recv, l_sem,
):
    rows, d = x.shape
    ff = wg.shape[1]
    half, nb = d // 2, d // 8
    hw = nb // 2
    steps_a, blocks, per = ff // NA, rows // BLOCK, BLOCK // CHUNK
    chunks = blocks * 4 * per
    d1, d2, d3, d4 = LAGS

    dp, me = lax.axis_index("dp"), lax.axis_index("tp")
    z, c = me // 2, me % 2
    inner = (z == 1) | (z == 2)
    outer = jnp.logical_not(inner)
    partner = me + 1 - 2 * c
    inward = (1 + z // 2) * 2 + c
    outward = (3 * (z - 1)) * 2 + c
    across = (3 - z) * 2 + c
    mine = pl.multiple_of(jnp.where(z == 2, hw, 0), hw)
    other = pl.multiple_of(hw - mine, hw)
    own0, par0 = c * half, (1 - c) * half

    def remote(src, dst, send, recv, to):
        return pltpu.make_async_remote_copy(
            src_ref=src, dst_ref=dst, send_sem=send, recv_sem=recv,
            device_id=(dp, to), device_id_type=MESH,
        )

    def place(u):
        b, i, r = u // (4 * per), (u // per) % 4, u % per
        return pl.ds(pl.multiple_of(b * BLOCK + r * CHUNK, CHUNK), CHUNK), i, pl.ds(pl.multiple_of(r * CHUNK, CHUNK), CHUNK)

    def cols(base, i, off, n):
        return pl.ds(pl.multiple_of(base + i * nb + off, n), n)

    def x_copy(b):
        return pltpu.make_async_copy(x.at[pl.ds(pl.multiple_of(b * BLOCK, BLOCK), BLOCK), :], xb, sx)

    def a_copies(n, s):
        col = pl.ds(pl.multiple_of(n * NA, NA), NA)
        return [pltpu.make_async_copy(w.at[:, col], wa.at[s, j], sa.at[s, j]) for j, w in enumerate((wg, wu))]

    def b_copy(base, i, s):
        return pltpu.make_async_copy(wd.at[:, cols(base, i, 0, nb)], wb.at[s], sb.at[s])

    def p_copy():
        return remote(psend, pbuf, p_send, p_recv, partner)

    def o_copy(b, i, r):
        rw = pl.ds(pl.multiple_of(b * BLOCK + r * CHUNK, CHUNK), CHUNK)
        return remote(
            sent.at[i, pl.ds(r * CHUNK, CHUNK), :], cin.at[rw, cols(0, i, 0, nb)],
            o_send.at[i], c_recv.at[(b * 4 + i) * per + r], inward,
        )

    def o_wait(i):
        remote(sent.at[i], cin.at[pl.ds(0, BLOCK), cols(0, i, 0, nb)], o_send.at[i], c_recv.at[0], inward).wait_send()

    def c_arrival(u):
        rw, i, _ = place(u)
        return remote(cin.at[rw, cols(0, i, 0, nb)], cin.at[rw, cols(0, i, 0, nb)], o_send.at[0], c_recv.at[u], outward)

    def c_load(u):
        rw, i, _ = place(u)
        return pltpu.make_async_copy(cin.at[rw, cols(0, i, 0, nb)], cload, l_sem.at[0])

    def x_cols(i):
        return pl.ds(pl.multiple_of(i * hw, hw), hw)

    def e_copy(u):
        rw, i, _ = place(u)
        return remote(xsend.at[u % 4], xin.at[rw, x_cols(i)], x_send.at[u % 4], x_recv.at[u], across)

    def x_load(u):
        rw, i, _ = place(u)
        return pltpu.make_async_copy(xin.at[rw, x_cols(i)], xload, l_sem.at[1])

    def t_copies(u):
        rw, i, _ = place(u)
        dst, s = y.at[rw, cols(own0, i, mine, hw)], u % 4
        src = tsend.at[s]
        return [
            remote(src, dst, t_send.at[s, 0], y_recv.at[0, u], outward),
            remote(src, dst, t_send.at[s, 1], y_recv.at[0, u], across),
            remote(src, dst, t_send.at[s, 2], yp_recv, partner),
            pltpu.make_async_copy(src, dst, t_send.at[s, 3]),
        ]

    def t_wait(u):
        for j, t in enumerate(t_copies(u)):
            t.wait_send() if j < 3 else t.wait()

    def hand_on(u):
        rw, i, _ = place(u)
        at = y.at[rw, cols(own0, i, other, hw)]
        return remote(at, at, f_send, y_recv.at[1, u], outward), remote(at, at, g_send, yp_recv, partner)

    def pass_over(u):
        rw, i, _ = place(u)
        at = y.at[rw, cols(own0, i, 0, nb)]
        return remote(at, at, g_send, yp_recv, partner)

    def y_arrival(u, kind, off):
        rw, i, _ = place(u)
        at = y.at[rw, cols(own0, i, off, hw)]
        return remote(at, at, f_send, y_recv.at[kind, u], across)

    def live(u):
        return (u >= 0) & (u < chunks)

    def before(k):
        u, v = k - d1, k - d2

        @pl.when(inner & live(u))
        def _():
            c_arrival(u).wait_recv()
            c_load(u).start()

        @pl.when(inner & live(v))
        def _():
            e_copy(v).wait_recv()
            x_load(v).start()

    def after(k):
        u, v, w, q = k - d1, k - d2, k - d3, k - d4

        @pl.when(inner & live(u))
        def _():
            @pl.when(u >= 4)
            def _():
                e_copy(u - 4).wait_send()

            _, i, r = place(u)
            c_load(u).wait()
            xsend[u % 4] = (part[i, r, pl.ds(other, hw)] + cload[:, pl.ds(other, hw)].astype(F32)).astype(BF16)
            e_copy(u).start()
            part[i, r, pl.ds(mine, hw)] += cload[:, pl.ds(mine, hw)].astype(F32)

        @pl.when(inner & live(v))
        def _():
            @pl.when(v >= 4)
            def _():
                t_wait(v - 4)

            _, i, r = place(v)
            x_load(v).wait()
            tsend[v % 4] = (part[i, r, pl.ds(mine, hw)] + xload[...].astype(F32)).astype(BF16)
            for t in t_copies(v):
                t.start()

        @pl.when(inner & live(w))
        def _():
            y_arrival(w, 0, other).wait_recv()
            for t in hand_on(w):
                t.start()

        @pl.when(outer & live(q))
        def _():
            near = pl.multiple_of(jnp.where(z == 3, hw, 0), hw)
            y_arrival(q, 0, near).wait_recv()
            y_arrival(q, 1, pl.multiple_of(hw - near, hw)).wait_recv()
            pass_over(q).start()

    barrier = pltpu.get_barrier_semaphore()
    pl.semaphore_signal(barrier, inc=1, device_id=(dp, partner), device_id_type=MESH)

    @pl.when(inner)
    def _():
        pl.semaphore_signal(barrier, inc=1, device_id=(dp, outward), device_id_type=MESH)
        pl.semaphore_signal(barrier, inc=1, device_id=(dp, across), device_id_type=MESH)
        pl.semaphore_wait(barrier, 3)

    @pl.when(outer)
    def _():
        pl.semaphore_signal(barrier, inc=1, device_id=(dp, inward), device_id_type=MESH)
        pl.semaphore_wait(barrier, 2)

    x_copy(0).start()
    for t in a_copies(0, 0):
        t.start()

    def block(b, _):
        x_copy(b).wait()

        def a_step(n, _):
            s, k = n % 2, b * 4 * per - steps_a + n

            @pl.when(n + 1 < steps_a)
            def _():
                for t in a_copies(n + 1, 1 - s):
                    t.start()

            @pl.when(n == steps_a - 1)
            def _():
                b_copy(par0, 0, 0).start()

            before(k)
            for t in a_copies(n, s):
                t.wait()
            gate = jnp.dot(xb[...], wa[s, 0], preferred_element_type=F32)
            up = jnp.dot(xb[...], wa[s, 1], preferred_element_type=F32)
            hb[:, pl.ds(pl.multiple_of(n * NA, NA), NA)] = (jax.nn.silu(gate) * up).astype(BF16)
            after(k)
            return 0

        lax.fori_loop(0, steps_a, a_step, 0)

        def b_step(i, _):
            k = b * 4 * per + i
            b_copy(own0, i, 1).start()

            @pl.when((i == 0) & (b + 1 < blocks))
            def _():
                x_copy(b + 1).start()

            b_copy(par0, i, 0).wait()
            count = b * 4 + i

            @pl.when(count > 0)
            def _():
                p_copy().wait_send()

            psend[...] = jnp.dot(hb[...], wb[0], preferred_element_type=F32).astype(BF16)

            @pl.when(count > 0)
            def _():
                pl.semaphore_wait(p_free, 1)

            p_copy().start()

            @pl.when(i < 3)
            def _():
                b_copy(par0, i + 1, 0).start()

            @pl.when((i == 3) & (b + 1 < blocks))
            def _():
                for t in a_copies(0, 0):
                    t.start()

            before(k)
            b_copy(own0, i, 1).wait()
            part[i] = jnp.dot(hb[...], wb[1], preferred_element_type=F32)
            p_copy().wait_recv()

            @pl.when(inner)
            def _():
                part[i] += pbuf[...].astype(F32)

            @pl.when(outer)
            def _():
                @pl.when(b > 0)
                def _():
                    o_wait(i)

                for r in range(per):
                    at = pl.ds(r * CHUNK, CHUNK)
                    sent[i, at, :] = (part[i, at, :] + pbuf[at, :].astype(F32)).astype(BF16)
                    o_copy(b, i, r).start()

            @pl.when(count < blocks * 4 - 1)
            def _():
                pl.semaphore_signal(p_free, inc=1, device_id=(dp, partner), device_id_type=MESH)

            after(k)
            return 0

        lax.fori_loop(0, 4, b_step, 0)
        return 0

    lax.fori_loop(0, blocks, block, 0)

    def drain(k, _):
        before(k)
        after(k)
        return 0

    lax.fori_loop(chunks - 4 * per + 4, chunks + d4, drain, 0)

    p_copy().wait_send()
    side = y.at[:, pl.ds(0, half)]
    quarter = y.at[:, pl.ds(0, half // 2)]

    @pl.when(outer)
    def _():
        for i in range(4):
            o_wait(i)
        remote(side, side, g_send, yp_recv, partner).wait_send()

    @pl.when(inner)
    def _():
        for s in range(4):
            e_copy(chunks - 4 + s).wait_send()
            t_wait(chunks - 4 + s)
        remote(quarter, quarter, f_send, yp_recv, partner).wait_send()
        remote(quarter, quarter, g_send, yp_recv, partner).wait_send()

    remote(side, side, g_send, yp_recv, partner).wait_recv()


def block_call(x, wg, wu, wd):
    rows, d = x.shape
    ff = wg.shape[1]
    half, nb = d // 2, d // 8
    hw = nb // 2
    chunks = (rows // BLOCK) * 4 * (BLOCK // CHUNK)
    dma, any_ = pltpu.SemaphoreType.DMA, pl.BlockSpec(memory_space=pl.ANY)
    flops = 6 * rows * d * ff
    return pl.pallas_call(
        kernel,
        out_shape=[
            jax.ShapeDtypeStruct((rows, d), BF16),
            jax.ShapeDtypeStruct((rows, half), BF16),
            jax.ShapeDtypeStruct((rows, half // 2), BF16),
        ],
        in_specs=[any_] * 4,
        out_specs=[any_] * 3,
        scratch_shapes=[
            pltpu.VMEM((BLOCK, d), BF16),
            pltpu.VMEM((BLOCK, ff), BF16),
            pltpu.VMEM((2, 2, d, NA), BF16),
            pltpu.VMEM((2, ff, nb), BF16),
            pltpu.VMEM((4, BLOCK, nb), F32),
            pltpu.VMEM((4, BLOCK, nb), BF16),
            pltpu.VMEM((BLOCK, nb), BF16),
            pltpu.VMEM((BLOCK, nb), BF16),
            pltpu.VMEM((CHUNK, nb), BF16),
            pltpu.VMEM((CHUNK, hw), BF16),
            pltpu.VMEM((4, CHUNK, hw), BF16),
            pltpu.VMEM((4, CHUNK, hw), BF16),
            dma, dma((2, 2)), dma((2,)), dma, dma, pltpu.SemaphoreType.REGULAR,
            dma((4,)), dma((chunks,)), dma((4,)), dma((chunks,)),
            dma((4, 4)), dma((2, chunks)), dma, dma, dma, dma((2,)),
        ],
        compiler_params=pltpu.CompilerParams(collective_id=0, has_side_effects=True, vmem_limit_bytes=VMEM),
        cost_estimate=pl.CostEstimate(flops=flops, bytes_accessed=10**9, transcendentals=rows * ff),
        name="mlp_block",
    )(x, wg, wu, wd)[0]


def solution(mesh):
    return jax.shard_map(
        block_call,
        mesh=mesh,
        in_specs=(P("dp", None), P(None, "tp"), P(None, "tp"), P("tp", None)),
        out_specs=P("dp", None),
        check_vma=False,
    )
```

time: 1040 us -> 511 us (0.49)
  waiting for transfers between devices: 651 us -> 0 us
  Pallas kernels: 0 us -> 487 us
  matrix products: 352 us -> 0 us
  between operations: 13.4 us -> 0.01 us
    psum x1 -> x0, waiting for transfers between devices: 651 us -> none  [step(): return lax.psum(term, 'tp')]
    pallas_call x0 -> x1, Pallas kernels: none -> 487 us  [block_call(): pl.pallas_call(kernel, out_shape=[jax.ShapeDtypeStruct((rows, d), BF16),...]
    dot_general x3 -> x0, matrix products: 352 us -> none  [the longest x1 122 us: step(): up = jnp.dot(x, w_up, preferred_element_type=jnp.float32)]
  transfers between devices with their start and end apart: 1 -> 0, of which waited for: 1 -> 0; matrix products, arithmetic and copies ran while one was open for 0% -> 0% of each run, Pallas kernels for 0% -> 0%
where the time goes in v1:
time: 511 us; the launch traced here: 510 us
  Pallas kernels  487 us (95%)
  local copies, waits for them, and re-layouts  23 us (5%)
    pallas_call x1, Pallas kernels, block_call(): pl.pallas_call(kernel, out_shape=[jax.ShapeDtypeStruct((rows, d), BF16),...  487 us
    unnamed x1, local copies, waits for them, and re-layouts  23 us

profile of v1, /device:TPU:0, one launch (start us, length us, event | category | flops | bytes accessed | tf_op | source)
XLA Modules:
  0.0 510.1 jit_solution(16198471576986079500)
XLA Ops:
  0.0 487.1 %mlp_block.1 = (bf16[2048,8192]{1,0:T(8,128)(2,1)}, bf16[2048,4096]{1,0:T(8,128)(2,1)}, bf16[2048,2048]{1,0:T(8,128)(2,1)}) custom-call(bf16[2048,8192]{1,0:T(8,128)(2,1)} %x.1, bf16[8192,3072]{1,0:T(8,128)(2,1)} %wg.1, bf16[8192,3072]{1,0:T(8,128)(2,1)} %wu.1, bf16[3072,8192]{1,0:T(8,128)(2,1)} %wd.1), custom_call_target="tpu_custom_call" | custom-call | flops 309237645312 | bytes 1000000000 | tf_op jit(solution)/shard_map/mlp_block/pallas_call | solution.py:329
  487.1 23.0 %copy.6 = bf16[2048,8192]{1,0:T(8,128)(2,1)} copy(bf16[2048,8192]{1,0:T(8,128)(2,1)} %get-tuple-element.6) | data formatting | bytes 67108864

commit v2 on v1

v2 whole, which is shorter than its diff:
```python
import functools

import jax
import jax.numpy as jnp
from jax import lax
from jax.experimental import pallas as pl
from jax.experimental.pallas import tpu as pltpu
from jax.sharding import PartitionSpec as P

MESH = pl.DeviceIdType.MESH
BF16, F32 = jnp.bfloat16, jnp.float32
BLOCK, CHUNK, NA = 384, 128, 256
BULK = 1
VMEM = 67043328
SLOTS, RING, DEEP = 8, 4, 3
STEP_A, STEP_B, DUE = 184, 144, 630
LAGS, BEHIND = (0, 2, 5), 16


def kernel(
    x, wg, wu, wd,
    y, cin,
    xb, hb, wa, wb, part, sent, psend, pbuf, cload, xin, xsend, tsend,
    sx, sa, sb, p_send, p_recv, p_free, o_send, c_recv, x_send, x_recv,
    t_send, y_recv, f_send, g_send, yp_recv, l_sem,
):
    rows, d = x.shape
    ff = wg.shape[1]
    half, nb = d // 2, d // 8
    hw = nb // 2
    steps_a, whole, per = ff // NA, rows // BLOCK, BLOCK // CHUNK
    tail = rows - whole * BLOCK
    blocks, chunks, per_tail = whole + (tail > 0), rows // CHUNK * 4, max(tail // CHUNK, 1)
    tick = (8 * STEP_B + steps_a * STEP_A) // (4 * per)

    dp, me = lax.axis_index("dp"), lax.axis_index("tp")
    z, c = me // 2, me % 2
    inner = (z == 1) | (z == 2)
    outer = jnp.logical_not(inner)
    partner = me + 1 - 2 * c
    inward = (1 + z // 2) * 2 + c
    outward = (3 * (z - 1)) * 2 + c
    across = (3 - z) * 2 + c
    mine = pl.multiple_of(jnp.where(z == 2, hw, 0), hw)
    other = pl.multiple_of(hw - mine, hw)
    own0, par0 = c * half, (1 - c) * half

    def remote(src, dst, send, recv, to):
        return pltpu.make_async_remote_copy(
            src_ref=src, dst_ref=dst, send_sem=send, recv_sem=recv,
            device_id=(dp, to), device_id_type=MESH,
        )

    def place(u):
        b, w = lax.div(u, 4 * per), lax.rem(u, 4 * per)
        n = jnp.where(b < whole, per, per_tail)
        i = jnp.where(b < whole, lax.div(w, per), lax.div(w, per_tail))
        r = w - i * n
        return (
            pl.ds(pl.multiple_of(b * BLOCK + r * CHUNK, CHUNK), CHUNK), i, pl.ds(pl.multiple_of(r * CHUNK, CHUNK), CHUNK)
        )

    def cols(base, i, off, n):
        return pl.ds(pl.multiple_of(base + i * nb + off, n), n)

    def x_copy(b, m):
        return pltpu.make_async_copy(x.at[pl.ds(pl.multiple_of(b * BLOCK, CHUNK), m), :], xb.at[pl.ds(0, m), :], sx)

    def a_copies(n, s):
        col = pl.ds(pl.multiple_of(n * NA, NA), NA)
        return [pltpu.make_async_copy(w.at[:, col], wa.at[s, j], sa.at[s, j]) for j, w in enumerate((wg, wu))]

    def b_copy(base, i, s):
        return pltpu.make_async_copy(wd.at[:, cols(base, i, 0, nb)], wb.at[s], sb.at[s])

    def p_copy(m):
        return remote(psend.at[pl.ds(0, m), :], pbuf.at[pl.ds(0, m), :], p_send, p_recv, partner)

    def o_copy(b, i, r, u):
        rw = pl.ds(pl.multiple_of(b * BLOCK + r * CHUNK, CHUNK), CHUNK)
        return remote(
            sent.at[i, pl.ds(r * CHUNK, CHUNK), :], cin.at[rw, cols(0, i, 0, nb)],
            o_send.at[i], c_recv.at[u], inward,
        )

    def o_wait(i, m):
        at = pl.ds(0, m)
        remote(sent.at[i, at, :], cin.at[at, cols(0, i, 0, nb)], o_send.at[i], c_recv.at[0], inward).wait_send()

    def c_arrival(u):
        rw, i, _ = place(u)
        return remote(cin.at[rw, cols(0, i, 0, nb)], cin.at[rw, cols(0, i, 0, nb)], o_send.at[0], c_recv.at[u], outward)

    def c_load(u):
        rw, i, _ = place(u)
        return pltpu.make_async_copy(cin.at[rw, cols(0, i, 0, nb)], cload.at[lax.rem(u, 2)], l_sem.at[lax.rem(u, 2)])

    def e_copy(u):
        return remote(xsend.at[lax.rem(u, RING)], xin.at[lax.rem(u, SLOTS)], x_send.at[lax.rem(u, RING)], x_recv.at[lax.rem(u, SLOTS)], across)

    def t_copies(u):
        rw, i, _ = place(u)
        dst, s = y.at[rw, cols(own0, i, mine, hw)], lax.rem(u, RING)
        src = tsend.at[s]
        return [
            remote(src, dst, t_send.at[s, 0], y_recv.at[0, u], outward),
            remote(src, dst, t_send.at[s, 1], y_recv.at[0, u], across),
            remote(src, dst, t_send.at[s, 2], yp_recv, partner),
            pltpu.make_async_copy(src, dst, t_send.at[s, 3]),
        ]

    def t_wait(u):
        for j, t in enumerate(t_copies(u)):
            t.wait_send() if j < 3 else t.wait()

    def hand_on(u):
        rw, i, _ = place(u)
        at = y.at[rw, cols(own0, i, other, hw)]
        return remote(at, at, f_send, y_recv.at[1, u], outward), remote(at, at, g_send, yp_recv, partner)

    def pass_over(u):
        rw, i, _ = place(u)
        at = y.at[rw, cols(own0, i, 0, nb)]
        return remote(at, at, g_send, yp_recv, partner)

    def y_arrival(u, kind, off):
        rw, i, _ = place(u)
        at = y.at[rw, cols(own0, i, off, hw)]
        return remote(at, at, f_send, y_recv.at[kind, u], across)

    def advance(clock, step):
        t, due, *made = clock
        t = t + step
        on = jnp.where(t >= due, 1, 0)
        return (t, due + tick * on, made[0] + on, *made[:-1])

    def turn(clock, stage):
        made = clock[2:]
        lag, behind = (LAGS[stage], 0) if stage < 3 else (0, BEHIND)
        u = made[lag + 1] - behind
        return u, (made[lag] > made[lag + 1]) & (u >= 0) & (u < chunks)

    def before(clock):
        def fetch(u):
            c_arrival(u).wait_recv()
            c_load(u).start()

        u, on = turn(clock, 0)
        pl.when(inner & on)(functools.partial(fetch, u))

    def add_outer(u):
        @pl.when(u >= RING)
        def _():
            e_copy(u - RING).wait_send()

        _, i, r = place(u)
        c_load(u).wait()
        got = cload.at[lax.rem(u, 2)]
        xsend[lax.rem(u, RING)] = (part[i, r, pl.ds(other, hw)] + got[:, pl.ds(other, hw)].astype(F32)).astype(BF16)
        e_copy(u).start()
        part[i, r, pl.ds(mine, hw)] += got[:, pl.ds(mine, hw)].astype(F32)

    def add_across(u):
        @pl.when(u >= RING)
        def _():
            t_wait(u - RING)

        _, i, r = place(u)
        e_copy(u).wait_recv()
        tsend[lax.rem(u, RING)] = (part[i, r, pl.ds(mine, hw)] + xin[lax.rem(u, SLOTS)].astype(F32)).astype(BF16)
        for t in t_copies(u):
            t.start()

    def pass_outward(u):
        y_arrival(u, 0, other).wait_recv()
        for t in hand_on(u):
            t.start()

    def pass_across(u):
        near = pl.multiple_of(jnp.where(z == 3, hw, 0), hw)
        y_arrival(u, 0, near).wait_recv()
        y_arrival(u, 1, pl.multiple_of(hw - near, hw)).wait_recv()
        pass_over(u).start()

    def after(clock):
        for stage, (role, work) in enumerate(
            ((inner, add_outer), (inner, add_across), (inner, pass_outward), (outer, pass_across))
        ):
            u, on = turn(clock, stage)
            pl.when(role & on)(functools.partial(work, u))

    x_copy(0, BLOCK).start(priority=BULK)
    for t in a_copies(0, 0):
        t.start(priority=BULK)

    barrier = pltpu.get_barrier_semaphore()
    pl.semaphore_signal(barrier, inc=1, device_id=(dp, partner), device_id_type=MESH)

    @pl.when(inner)
    def _():
        pl.semaphore_signal(barrier, inc=1, device_id=(dp, outward), device_id_type=MESH)
        pl.semaphore_signal(barrier, inc=1, device_id=(dp, across), device_id_type=MESH)

    @pl.when(outer)
    def _():
        pl.semaphore_signal(barrier, inc=1, device_id=(dp, inward), device_id_type=MESH)

    def next_x(b):
        @pl.when(b + 1 < whole)
        def _():
            x_copy(b + 1, BLOCK).start(priority=BULK)

        if tail:
            @pl.when(b + 1 == whole)
            def _():
                x_copy(b + 1, tail).start(priority=BULK)

    def block(b, m, clock):
        x_copy(b, m).wait()
        mine_rows = pl.ds(0, m)

        @pl.when(b == 0)
        def _():
            for n in range(1, DEEP - 1):
                for t in a_copies(n, n):
                    t.start(priority=BULK)

        def a_step(n, clock):
            s, clock = lax.rem(n, DEEP), advance(clock, STEP_A)

            @pl.when(n + DEEP - 1 < steps_a)
            def _():
                for t in a_copies(n + DEEP - 1, lax.rem(n + DEEP - 1, DEEP)):
                    t.start(priority=BULK)

            @pl.when(n == steps_a - 1)
            def _():
                b_copy(par0, 0, 0).start(priority=BULK)
                b_copy(own0, 0, 1).start(priority=BULK)

            @pl.when((b == 0) & (n == steps_a - 1) & inner)
            def _():
                pl.semaphore_wait(barrier, 3)

            @pl.when((b == 0) & (n == steps_a - 1) & outer)
            def _():
                pl.semaphore_wait(barrier, 2)

            before(clock)
            for t in a_copies(n, s):
                t.wait()
            gate = jnp.dot(xb[mine_rows, :], wa[s, 0], preferred_element_type=F32)
            up = jnp.dot(xb[mine_rows, :], wa[s, 1], preferred_element_type=F32)
            hb[mine_rows, pl.ds(pl.multiple_of(n * NA, NA), NA)] = (jax.nn.silu(gate) * up).astype(BF16)
            after(clock)
            return clock

        clock = lax.fori_loop(0, steps_a, a_step, clock)
        next_x(b)

        def b_step(i, clock):
            clock, count = advance(clock, STEP_B), b * 4 + i
            b_copy(par0, i, 0).wait()

            @pl.when((count > 0) & (i > 0))
            def _():
                p_copy(m).wait_send()

            @pl.when((count > 0) & (i == 0))
            def _():
                p_copy(BLOCK).wait_send()

            before(clock)
            psend[mine_rows, :] = jnp.dot(hb[mine_rows, :], wb[0], preferred_element_type=F32).astype(BF16)

            @pl.when(count > 0)
            def _():
                pl.semaphore_wait(p_free, 1)

            p_copy(m).start()

            @pl.when(i < 3)
            def _():
                b_copy(par0, i + 1, 0).start(priority=BULK)

            @pl.when((i >= 5 - DEEP) & (b + 1 < blocks))
            def _():
                for t in a_copies(i - (5 - DEEP), i - (5 - DEEP)):
                    t.start(priority=BULK)

            after(clock)
            clock = advance(clock, STEP_B)
            before(clock)
            b_copy(own0, i, 1).wait()
            part[i, mine_rows, :] = jnp.dot(hb[mine_rows, :], wb[1], preferred_element_type=F32)

            @pl.when(i < 3)
            def _():
                b_copy(own0, i + 1, 1).start(priority=BULK)

            p_copy(m).wait_recv()

            @pl.when(inner)
            def _():
                part[i, mine_rows, :] += pbuf[mine_rows, :].astype(F32)

            @pl.when(outer)
            def _():
                @pl.when(b > 0)
                def _():
                    o_wait(i, BLOCK)

                for r in range(m // CHUNK):
                    at = pl.ds(r * CHUNK, CHUNK)
                    sent[i, at, :] = (part[i, at, :] + pbuf[at, :].astype(F32)).astype(BF16)
                    o_copy(b, i, r, b * 4 * per + i * (m // CHUNK) + r).start()

            @pl.when(count < blocks * 4 - 1)
            def _():
                pl.semaphore_signal(p_free, inc=1, device_id=(dp, partner), device_id_type=MESH)

            after(clock)
            return clock

        return lax.fori_loop(0, 4, b_step, clock)

    clock = (-steps_a * STEP_A, DUE) + (0,) * (max(LAGS) + 2)
    clock = lax.fori_loop(0, whole, lambda b, clock: block(b, BLOCK, clock), tuple(jnp.int32(v) for v in clock))
    if tail:
        clock = block(whole, tail, clock)

    def drain(_, clock):
        clock = advance(clock, tick)
        before(clock)
        after(clock)
        return clock

    left = chunks + max(BEHIND, max(LAGS)) - ((blocks - 1) * 4 * per + (8 * STEP_B - DUE) // tick)
    lax.fori_loop(0, left, drain, clock)

    p_copy(tail or BLOCK).wait_send()
    side = y.at[:, pl.ds(0, half)]
    quarter = y.at[:, pl.ds(0, half // 2)]

    @pl.when(outer)
    def _():
        for i in range(4):
            o_wait(i, tail or BLOCK)
        remote(side, side, g_send, yp_recv, partner).wait_send()

    @pl.when(inner)
    def _():
        for s in range(RING):
            e_copy(chunks - RING + s).wait_send()
            t_wait(chunks - RING + s)
        remote(quarter, quarter, f_send, yp_recv, partner).wait_send()
        remote(quarter, quarter, g_send, yp_recv, partner).wait_send()

    remote(side, side, g_send, yp_recv, partner).wait_recv()


def block_call(x, wg, wu, wd):
    rows, d = x.shape
    ff = wg.shape[1]
    half, nb = d // 2, d // 8
    hw = nb // 2
    chunks = rows // CHUNK * 4
    dma, any_ = pltpu.SemaphoreType.DMA, pl.BlockSpec(memory_space=pl.ANY)
    flops = 6 * rows * d * ff
    return pl.pallas_call(
        kernel,
        out_shape=[
            jax.ShapeDtypeStruct((rows, d), BF16),
            jax.ShapeDtypeStruct((rows, half), BF16),
        ],
        in_specs=[any_] * 4,
        out_specs=[any_] * 2,
        scratch_shapes=[
            pltpu.VMEM((BLOCK, d), BF16),
            pltpu.VMEM((BLOCK, ff), BF16),
            pltpu.VMEM((DEEP, 2, d, NA), BF16),
            pltpu.VMEM((2, ff, nb), BF16),
            pltpu.VMEM((4, BLOCK, nb), F32),
            pltpu.VMEM((4, BLOCK, nb), BF16),
            pltpu.VMEM((BLOCK, nb), BF16),
            pltpu.VMEM((BLOCK, nb), BF16),
            pltpu.VMEM((2, CHUNK, nb), BF16),
            pltpu.VMEM((SLOTS, CHUNK, hw), BF16),
            pltpu.VMEM((RING, CHUNK, hw), BF16),
            pltpu.VMEM((RING, CHUNK, hw), BF16),
            dma, dma((DEEP, 2)), dma((2,)), dma, dma, pltpu.SemaphoreType.REGULAR,
            dma((4,)), dma((chunks,)), dma((RING,)), dma((SLOTS,)),
            dma((RING, 4)), dma((2, chunks)), dma, dma, dma, dma((2,)),
        ],
        compiler_params=pltpu.CompilerParams(collective_id=0, has_side_effects=True, vmem_limit_bytes=VMEM),
        cost_estimate=pl.CostEstimate(flops=flops, bytes_accessed=10**9, transcendentals=rows * ff),
        name="mlp_block",
    )(x, wg, wu, wd)[0]


def solution(mesh):
    return jax.shard_map(
        block_call,
        mesh=mesh,
        in_specs=(P("dp", None), P(None, "tp"), P(None, "tp"), P("tp", None)),
        out_specs=P("dp", None),
        check_vma=False,
    )
```

time: 511 us -> 475 us (0.930)
  Pallas kernels: 487 us -> 452 us
    pallas_call x1, Pallas kernels: 487 us -> 452 us  [block_call(): pl.pallas_call(kernel, out_shape=[jax.ShapeDtypeStruct((rows, d), BF16),...]
where the time goes in v2:
time: 475 us
  Pallas kernels  452 us (95%)
  local copies, waits for them, and re-layouts  23 us (5%)
    pallas_call x1, Pallas kernels, block_call(): pl.pallas_call(kernel, out_shape=[jax.ShapeDtypeStruct((rows, d), BF16),...  452 us
    unnamed x1, local copies, waits for them, and re-layouts  23 us

profile of v2, /device:TPU:0, one launch (start us, length us, event | category | flops | bytes accessed | tf_op | source)
XLA Modules:
  0.0 475.1 jit_solution(9313490157233299641)
XLA Ops:
  0.0 452.1 %mlp_block.1 = (bf16[2048,8192]{1,0:T(8,128)(2,1)}, bf16[2048,4096]{1,0:T(8,128)(2,1)}) custom-call(bf16[2048,8192]{1,0:T(8,128)(2,1)} %x.1, bf16[8192,3072]{1,0:T(8,128)(2,1)} %wg.1, bf16[8192,3072]{1,0:T(8,128)(2,1)} %wu.1, bf16[3072,8192]{1,0:T(8,128)(2,1)} %wd.1), custom_call_target="tpu_custom_call" | custom-call | flops 309237645312 | bytes 1000000000 | tf_op jit(solution)/shard_map/mlp_block/pallas_call | solution.py:370
  452.1 23.0 %copy.6 = bf16[2048,8192]{1,0:T(8,128)(2,1)} copy(bf16[2048,8192]{1,0:T(8,128)(2,1)} %get-tuple-element.6) | data formatting | bytes 67108864

commit v3 on v2

--- a/solution.py
+++ b/solution.py
@@ -11,15 +11,18 @@
 BF16, F32 = jnp.bfloat16, jnp.float32
 BLOCK, CHUNK, NA = 384, 128, 256
 BULK = 1
+FIRST, COPY_FLOPS = 11, 10**9
+LATE = 2
 VMEM = 67043328
 SLOTS, RING, DEEP = 8, 4, 3
-STEP_A, STEP_B, DUE = 184, 144, 630
+STEP_A, STEP_B, DUE, TICK = 184, 144, 700, 270
+TAIL_A, TAIL_B = 130, 94
 LAGS, BEHIND = (0, 2, 5), 16
 
 
 def kernel(
     x, wg, wu, wd,
-    y, cin,
+    y, cin, late,
     xb, hb, wa, wb, part, sent, psend, pbuf, cload, xin, xsend, tsend,
     sx, sa, sb, p_send, p_recv, p_free, o_send, c_recv, x_send, x_recv,
     t_send, y_recv, f_send, g_send, yp_recv, l_sem,
@@ -31,7 +34,7 @@
     steps_a, whole, per = ff // NA, rows // BLOCK, BLOCK // CHUNK
     tail = rows - whole * BLOCK
     blocks, chunks, per_tail = whole + (tail > 0), rows // CHUNK * 4, max(tail // CHUNK, 1)
-    tick = (8 * STEP_B + steps_a * STEP_A) // (4 * per)
+    tick = TICK
 
     dp, me = lax.axis_index("dp"), lax.axis_index("tp")
     z, c = me // 2, me % 2
@@ -43,6 +46,7 @@
     across = (3 - z) * 2 + c
     mine = pl.multiple_of(jnp.where(z == 2, hw, 0), hw)
     other = pl.multiple_of(hw - mine, hw)
+    near = pl.multiple_of(jnp.where(z == 3, hw, 0), hw)
     own0, par0 = c * half, (1 - c) * half
 
     def remote(src, dst, send, recv, to):
@@ -76,24 +80,30 @@
     def p_copy(m):
         return remote(psend.at[pl.ds(0, m), :], pbuf.at[pl.ds(0, m), :], p_send, p_recv, partner)
 
-    def o_copy(b, i, r, u):
+    def o_copies(b, i, r, u):
         rw = pl.ds(pl.multiple_of(b * BLOCK + r * CHUNK, CHUNK), CHUNK)
-        return remote(
-            sent.at[i, pl.ds(r * CHUNK, CHUNK), :], cin.at[rw, cols(0, i, 0, nb)],
-            o_send.at[i], c_recv.at[u], inward,
-        )
+        return [
+            remote(
+                sent.at[i, pl.ds(r * CHUNK, CHUNK), pl.ds(off, hw)], cin.at[rw, cols(0, i, off, hw)],
+                o_send.at[i], c_recv.at[j, u], inward,
+            )
+            for j, off in enumerate((pl.multiple_of(hw - near, hw), near))
+        ]
 
     def o_wait(i, m):
         at = pl.ds(0, m)
-        remote(sent.at[i, at, :], cin.at[at, cols(0, i, 0, nb)], o_send.at[i], c_recv.at[0], inward).wait_send()
-
-    def c_arrival(u):
+        remote(sent.at[i, at, :], cin.at[at, cols(0, i, 0, nb)], o_send.at[i], c_recv.at[0, 0], inward).wait_send()
+
+    def c_half(u, j):
         rw, i, _ = place(u)
-        return remote(cin.at[rw, cols(0, i, 0, nb)], cin.at[rw, cols(0, i, 0, nb)], o_send.at[0], c_recv.at[u], outward)
-
-    def c_load(u):
-        rw, i, _ = place(u)
-        return pltpu.make_async_copy(cin.at[rw, cols(0, i, 0, nb)], cload.at[lax.rem(u, 2)], l_sem.at[lax.rem(u, 2)])
+        return cin.at[rw, cols(0, i, (other, mine)[j], hw)]
+
+    def c_arrival(u, j):
+        return remote(c_half(u, j), c_half(u, j), o_send.at[0], c_recv.at[j, u], outward)
+
+    def c_load(u, j):
+        s = lax.rem(u, 2)
+        return pltpu.make_async_copy(c_half(u, j), cload.at[j, s], l_sem.at[j, s])
 
     def e_copy(u):
         return remote(xsend.at[lax.rem(u, RING)], xin.at[lax.rem(u, SLOTS)], x_send.at[lax.rem(u, RING)], x_recv.at[lax.rem(u, SLOTS)], across)
@@ -110,8 +120,11 @@
         ]
 
     def t_wait(u):
-        for j, t in enumerate(t_copies(u)):
-            t.wait_send() if j < 3 else t.wait()
+        near_copy, *others, here = t_copies(u)
+        pl.when(u < chunks - LATE)(near_copy.wait_send)
+        for t in others:
+            t.wait_send()
+        here.wait()
 
     def hand_on(u):
         rw, i, _ = place(u)
@@ -138,15 +151,16 @@
         made = clock[2:]
         lag, behind = (LAGS[stage], 0) if stage < 3 else (0, BEHIND)
         u = made[lag + 1] - behind
-        return u, (made[lag] > made[lag + 1]) & (u >= 0) & (u < chunks)
+        return u, (made[lag] > made[lag + 1]) & (u >= 0) & (u < chunks - LATE * (stage == 3))
 
     def before(clock):
-        def fetch(u):
-            c_arrival(u).wait_recv()
-            c_load(u).start()
-
-        u, on = turn(clock, 0)
-        pl.when(inner & on)(functools.partial(fetch, u))
+        def fetch(u, j):
+            c_arrival(u, j).wait_recv()
+            c_load(u, j).start()
+
+        for j in (0, 1):
+            u, on = turn(clock, j)
+            pl.when(inner & on)(functools.partial(fetch, u, j))
 
     def add_outer(u):
         @pl.when(u >= RING)
@@ -154,11 +168,9 @@
             e_copy(u - RING).wait_send()
 
         _, i, r = place(u)
-        c_load(u).wait()
-        got = cload.at[lax.rem(u, 2)]
-        xsend[lax.rem(u, RING)] = (part[i, r, pl.ds(other, hw)] + got[:, pl.ds(other, hw)].astype(F32)).astype(BF16)
+        c_load(u, 0).wait()
+        xsend[lax.rem(u, RING)] = (part[i, r, pl.ds(other, hw)] + cload[0, lax.rem(u, 2)].astype(F32)).astype(BF16)
         e_copy(u).start()
-        part[i, r, pl.ds(mine, hw)] += got[:, pl.ds(mine, hw)].astype(F32)
 
     def add_across(u):
         @pl.when(u >= RING)
@@ -166,18 +178,22 @@
             t_wait(u - RING)
 
         _, i, r = place(u)
+        c_load(u, 1).wait()
+        here = part[i, r, pl.ds(mine, hw)] + cload[1, lax.rem(u, 2)].astype(F32)
         e_copy(u).wait_recv()
-        tsend[lax.rem(u, RING)] = (part[i, r, pl.ds(mine, hw)] + xin[lax.rem(u, SLOTS)].astype(F32)).astype(BF16)
-        for t in t_copies(u):
+        tsend[lax.rem(u, RING)] = (here + xin[lax.rem(u, SLOTS)].astype(F32)).astype(BF16)
+        near_copy, *others = t_copies(u)
+        pl.when(u < chunks - LATE)(near_copy.start)
+        for t in others:
             t.start()
 
     def pass_outward(u):
         y_arrival(u, 0, other).wait_recv()
-        for t in hand_on(u):
-            t.start()
+        out, over = hand_on(u)
+        pl.when(u < chunks - LATE)(out.start)
+        over.start()
 
     def pass_across(u):
-        near = pl.multiple_of(jnp.where(z == 3, hw, 0), hw)
         y_arrival(u, 0, near).wait_recv()
         y_arrival(u, 1, pl.multiple_of(hw - near, hw)).wait_recv()
         pass_over(u).start()
@@ -215,7 +231,7 @@
             def _():
                 x_copy(b + 1, tail).start(priority=BULK)
 
-    def block(b, m, clock):
+    def block(b, m, clock, long_a, long_b):
         x_copy(b, m).wait()
         mine_rows = pl.ds(0, m)
 
@@ -226,7 +242,7 @@
                     t.start(priority=BULK)
 
         def a_step(n, clock):
-            s, clock = lax.rem(n, DEEP), advance(clock, STEP_A)
+            s, clock = lax.rem(n, DEEP), advance(clock, long_a)
 
             @pl.when(n + DEEP - 1 < steps_a)
             def _():
@@ -259,7 +275,7 @@
         next_x(b)
 
         def b_step(i, clock):
-            clock, count = advance(clock, STEP_B), b * 4 + i
+            clock, count = advance(clock, long_b), b * 4 + i
             b_copy(par0, i, 0).wait()
 
             @pl.when((count > 0) & (i > 0))
@@ -289,7 +305,7 @@
                     t.start(priority=BULK)
 
             after(clock)
-            clock = advance(clock, STEP_B)
+            clock = advance(clock, long_b)
             before(clock)
             b_copy(own0, i, 1).wait()
             part[i, mine_rows, :] = jnp.dot(hb[mine_rows, :], wb[1], preferred_element_type=F32)
@@ -313,7 +329,8 @@
                 for r in range(m // CHUNK):
                     at = pl.ds(r * CHUNK, CHUNK)
                     sent[i, at, :] = (part[i, at, :] + pbuf[at, :].astype(F32)).astype(BF16)
-                    o_copy(b, i, r, b * 4 * per + i * (m // CHUNK) + r).start()
+                    for o in o_copies(b, i, r, b * 4 * per + i * (m // CHUNK) + r):
+                        o.start()
 
             @pl.when(count < blocks * 4 - 1)
             def _():
@@ -325,9 +342,9 @@
         return lax.fori_loop(0, 4, b_step, clock)
 
     clock = (-steps_a * STEP_A, DUE) + (0,) * (max(LAGS) + 2)
-    clock = lax.fori_loop(0, whole, lambda b, clock: block(b, BLOCK, clock), tuple(jnp.int32(v) for v in clock))
+    clock = lax.fori_loop(0, whole, lambda b, clock: block(b, BLOCK, clock, STEP_A, STEP_B), tuple(jnp.int32(v) for v in clock))
     if tail:
-        clock = block(whole, tail, clock)
+        clock = block(whole, tail, clock, TAIL_A, TAIL_B)
 
     def drain(_, clock):
         clock = advance(clock, tick)
@@ -335,28 +352,91 @@
         after(clock)
         return clock
 
-    left = chunks + max(BEHIND, max(LAGS)) - ((blocks - 1) * 4 * per + (8 * STEP_B - DUE) // tick)
+    end = (whole - 1) * (steps_a * STEP_A + 8 * STEP_B) + 8 * STEP_B + (tail > 0) * (steps_a * TAIL_A + 8 * TAIL_B)
+    left = chunks + max(BEHIND, max(LAGS)) - (end - DUE) // tick
     lax.fori_loop(0, left, drain, clock)
 
     p_copy(tail or BLOCK).wait_send()
-    side = y.at[:, pl.ds(0, half)]
-    quarter = y.at[:, pl.ds(0, half // 2)]
+
+    def bytes_of(count, columns):
+        return y.at[pl.ds(0, count * CHUNK * columns // d), :]
+
+    early = chunks - LATE
 
     @pl.when(outer)
     def _():
         for i in range(4):
             o_wait(i, tail or BLOCK)
-        remote(side, side, g_send, yp_recv, partner).wait_send()
+        passed = bytes_of(early, nb)
+        remote(passed, passed, g_send, yp_recv, partner).wait_send()
+        remote(passed, passed, g_send, yp_recv, partner).wait_recv()
 
     @pl.when(inner)
     def _():
         for s in range(RING):
             e_copy(chunks - RING + s).wait_send()
             t_wait(chunks - RING + s)
-        remote(quarter, quarter, f_send, yp_recv, partner).wait_send()
-        remote(quarter, quarter, g_send, yp_recv, partner).wait_send()
-
-    remote(side, side, g_send, yp_recv, partner).wait_recv()
+        out, over, took = bytes_of(early, hw), bytes_of(chunks, hw), bytes_of(chunks, nb)
+        remote(out, out, f_send, yp_recv, partner).wait_send()
+        remote(over, over, g_send, yp_recv, partner).wait_send()
+        remote(took, took, g_send, yp_recv, partner).wait_recv()
+        moves = []
+        for s in range(late.shape[1] // hw):
+            src = y.at[pl.ds(rows - CHUNK, CHUNK), pl.ds(pl.multiple_of(own0 + half - late.shape[1] + s * hw, hw), hw)]
+            moves.append((
+                pltpu.make_async_copy(src, tsend.at[s], t_send.at[s, 0]),
+                pltpu.make_async_copy(tsend.at[s], late.at[:, pl.ds(s * hw, hw)], t_send.at[s, 1]),
+            ))
+        for read, _ in moves:
+            read.start()
+        for read, write in moves:
+            read.wait()
+            write.start()
+        for _, write in moves:
+            write.wait()
+
+
+def copy_rows(first, count, src, *refs):
+    dst, held, read, written = refs[-4:]
+
+    def move(k):
+        rows = pl.ds((first + k) * CHUNK, CHUNK)
+        return (
+            pltpu.make_async_copy(src.at[rows, :], held.at[k], read.at[k]),
+            pltpu.make_async_copy(held.at[k], dst.at[rows, :], written.at[k]),
+        )
+
+    for k in range(count):
+        move(k)[0].start()
+    for k in range(count):
+        move(k)[0].wait()
+        move(k)[1].start()
+    for k in range(count):
+        move(k)[1].wait()
+
+
+def add_late(y_in, own, par, y, held, read, written):
+    rows, d = y.shape
+    me = lax.axis_index("tp")
+    z, c = me // 2, me % 2
+    wide = own.shape[1]
+
+    @pl.when((z == 0) | (z == 3))
+    def _():
+        moves = []
+        for j, (src, side) in enumerate(((own, c), (par, 1 - c))):
+            to = y.at[pl.ds(rows - CHUNK, CHUNK), pl.ds(pl.multiple_of(side * (d // 2) + d // 2 - wide, wide), wide)]
+            moves.append((
+                pltpu.make_async_copy(src, held.at[j], read.at[j]),
+                pltpu.make_async_copy(held.at[j], to, written.at[j]),
+            ))
+        for r, _ in moves:
+            r.start()
+        for r, w in moves:
+            r.wait()
+            w.start()
+        for _, w in moves:
+            w.wait()
 
 
 def block_call(x, wg, wu, wd):
@@ -367,14 +447,15 @@
     chunks = rows // CHUNK * 4
     dma, any_ = pltpu.SemaphoreType.DMA, pl.BlockSpec(memory_space=pl.ANY)
     flops = 6 * rows * d * ff
-    return pl.pallas_call(
+    summed, _, late = pl.pallas_call(
         kernel,
         out_shape=[
             jax.ShapeDtypeStruct((rows, d), BF16),
             jax.ShapeDtypeStruct((rows, half), BF16),
+            jax.ShapeDtypeStruct((CHUNK, LATE * nb), BF16),
         ],
         in_specs=[any_] * 4,
-        out_specs=[any_] * 2,
+        out_specs=[any_] * 3,
         scratch_shapes=[
             pltpu.VMEM((BLOCK, d), BF16),
             pltpu.VMEM((BLOCK, ff), BF16),
@@ -384,18 +465,50 @@
             pltpu.VMEM((4, BLOCK, nb), BF16),
             pltpu.VMEM((BLOCK, nb), BF16),
             pltpu.VMEM((BLOCK, nb), BF16),
-            pltpu.VMEM((2, CHUNK, nb), BF16),
+            pltpu.VMEM((2, 2, CHUNK, hw), BF16),
             pltpu.VMEM((SLOTS, CHUNK, hw), BF16),
             pltpu.VMEM((RING, CHUNK, hw), BF16),
             pltpu.VMEM((RING, CHUNK, hw), BF16),
             dma, dma((DEEP, 2)), dma((2,)), dma, dma, pltpu.SemaphoreType.REGULAR,
-            dma((4,)), dma((chunks,)), dma((RING,)), dma((SLOTS,)),
-            dma((RING, 4)), dma((2, chunks)), dma, dma, dma, dma((2,)),
+            dma((4,)), dma((2, chunks)), dma((RING,)), dma((SLOTS,)),
+            dma((RING, 4)), dma((2, chunks)), dma, dma, dma, dma((2, 2)),
         ],
         compiler_params=pltpu.CompilerParams(collective_id=0, has_side_effects=True, vmem_limit_bytes=VMEM),
         cost_estimate=pl.CostEstimate(flops=flops, bytes_accessed=10**9, transcendentals=rows * ff),
         name="mlp_block",
-    )(x, wg, wu, wd)[0]
+    )(x, wg, wu, wd)
+
+    wide = LATE * nb
+    own = lax.ppermute(late, "tp", [(2, 0), (3, 1), (4, 6), (5, 7)])
+    out = jax.ShapeDtypeStruct((rows, d), BF16)
+    params = pltpu.CompilerParams(vmem_limit_bytes=VMEM)
+
+    def copy_call(first, count, extra, alias, name):
+        return pl.pallas_call(
+            functools.partial(copy_rows, first, count),
+            out_shape=out,
+            in_specs=[any_] * (1 + len(extra)),
+            out_specs=any_,
+            scratch_shapes=[pltpu.VMEM((count, CHUNK, d), BF16), dma((count,)), dma((count,))],
+            input_output_aliases=alias,
+            compiler_params=params,
+            cost_estimate=pl.CostEstimate(flops=count * COPY_FLOPS, bytes_accessed=count * CHUNK * d * 4, transcendentals=0),
+            name=name,
+        )(summed, *extra)
+
+    own, y = lax.optimization_barrier((own, copy_call(0, FIRST, (), {}, "copy_first")))
+    par = lax.ppermute(own, "tp", [(0, 1), (1, 0), (6, 7), (7, 6)])
+    y = copy_call(FIRST, rows // CHUNK - FIRST, (own, y), {2: 0}, "copy_rest")
+    return pl.pallas_call(
+        add_late,
+        out_shape=out,
+        in_specs=[any_] * 3,
+        out_specs=any_,
+        scratch_shapes=[pltpu.VMEM((2, CHUNK, wide), BF16), dma((2,)), dma((2,))],
+        input_output_aliases={0: 0},
+        compiler_params=params,
+        name="late_chunks",
+    )(y, own, par)
 
 
 def solution(mesh):

time: 475 us -> 468 us (0.985)
  local copies, waits for them, and re-layouts: 23 us -> 0 us
  Pallas kernels: 452 us -> 464 us
    pallas_call x0 -> x3, Pallas kernels: none -> 25.5 us  [the longest x2 23.5 us: copy_call(): pl.pallas_call(functools.partial(copy_rows, first, count), out_shape=out,...]
    unnamed x1 -> x0, local copies, waits for them, and re-layouts: 23 us -> none
    pallas_call x1, Pallas kernels: 452 us -> 439 us  [block_call(): pl.pallas_call(kernel, out_shape=[jax.ShapeDtypeStruct((rows, d), BF16),...]
  transfers between devices with their start and end apart: 0 -> 2, of which waited for: 0 -> 0; matrix products, arithmetic and copies ran while one was open for 0% -> 0% of each run, Pallas kernels for 0% -> 5%
where the time goes in v3:
time: 468 us
  Pallas kernels  464 us (99%)
    pallas_call x1, Pallas kernels, block_call(): pl.pallas_call(kernel, out_shape=[jax.ShapeDtypeStruct((rows, d), BF16),...  439 us
    pallas_call x2, Pallas kernels, copy_call(): pl.pallas_call(functools.partial(copy_rows, first, count), out_shape=out,...  23.5 us
  transfers between devices with their start and end apart: 2, of which 0 were waited for; matrix products, arithmetic and copies ran while one was open for 0% of the time, Pallas kernels for 5%

profile of v3, /device:TPU:0, one launch (start us, length us, event | category | flops | bytes accessed | tf_op | source)
XLA Modules:
  0.0 467.7 jit_solution(1372073559264443701)
XLA Ops:
  0.0 438.5 %mlp_block.1 = (bf16[2048,8192]{1,0:T(8,128)(2,1)}, bf16[2048,4096]{1,0:T(8,128)(2,1)}, bf16[128,2048]{1,0:T(8,128)(2,1)}) custom-call(bf16[2048,8192]{1,0:T(8,128)(2,1)} %x.1, bf16[8192,3072]{1,0:T(8,128)(2,1)} %wg.1, bf16[8192,3072]{1,0:T(8,128)(2,1)} %wu.1, bf16[3072,8192]{1,0:T(8,128)(2,1)} %wd.1), custom_call_target="tpu_custom_call" | custom-call | flops 309237645312 | bytes 1000000000 | tf_op jit(solution)/shard_map/mlp_block/pallas_call | solution.py:450
  438.6 1.3 collective-permute-start
  439.9 15.8 %copy_first.1.refs_1_ = bf16[2048,8192]{1,0:T(8,128)(2,1)} custom-call(bf16[2048,8192]{1,0:T(8,128)(2,1)} %get-tuple-element.9.src), custom_call_target="tpu_custom_call" | custom-call | flops 11000000512 | bytes 46137344 | tf_op jit(solution)/shard_map/copy_first/pallas_call | solution.py:487
  455.7 0.0 collective-permute-done.refs_0_.own
  455.7 2.2 collective-permute-start.1
  457.9 7.7 %copy_rest.1.y_in = bf16[2048,8192]{1,0:T(8,128)(2,1)} custom-call(bf16[2048,8192]{1,0:T(8,128)(2,1)} %get-tuple-element.9.src, bf16[128,2048]{1,0:T(8,128)(2,1)} %collective-permute-done.refs_0_.own, bf16[2048,8192]{1,0:T(8,128)(2,1)} %copy_first.1.refs_1_), custom_call_target="tpu_custom_call", output_to_operand_aliasing={{}: (2, {})} | custom-call | flops 5000000000 | bytes 20971520 | tf_op jit(solution)/shard_map/copy_rest/pallas_call | solution.py:487
  465.6 0.0 collective-permute-done.1.par
  465.6 2.1 late_chunks.1
Async XLA Ops:
  438.6 17.1 %collective-permute-start = (bf16[128,2048]{1,0:T(8,128)(2,1)}, bf16[128,2048]{1,0:T(8,128)(2,1)}, u32[]{:S(2)}, u32[]{:S(2)}) collective-permute-start(bf16[128,2048]{1,0:T(8,128)(2,1)} %get-tuple-element.10), channel_id=1, source_target_pairs={{2,0},{3,1},{4,6},{5,7},{10,8},{11,9},{12,14},{13,15},{18,16},{19,... | collective-permute-start | bytes 1572872 | tf_op jit(solution)/shard_map/ppermute | solution.py:482
  455.7 9.9 %collective-permute-start.1 = (bf16[128,2048]{1,0:T(8,128)(2,1)}, bf16[128,2048]{1,0:T(8,128)(2,1)}, u32[]{:S(2)}, u32[]{:S(2)}) collective-permute-start(bf16[128,2048]{1,0:T(8,128)(2,1)} %collective-permute-done.refs_0_.own), channel_id=1, source_target_pairs={{0,1},{1,0},{6,7},{7,6},{8,9},{9,8},{14,15},{15,14},{16,17},{17,16... | collective-permute-start | bytes 1572872 | tf_op jit(solution)/shard_map/ppermute | solution.py:500

commit v4 on v3

--- a/solution.py
+++ b/solution.py
@@ -11,7 +11,7 @@
 BF16, F32 = jnp.bfloat16, jnp.float32
 BLOCK, CHUNK, NA = 384, 128, 256
 BULK = 1
-FIRST, COPY_FLOPS = 11, 10**9
+PIECE, FIRST, COPY_FLOPS = 32, 44, 25 * 10**7
 LATE = 2
 VMEM = 67043328
 SLOTS, RING, DEEP = 8, 4, 3
@@ -235,11 +235,9 @@
         x_copy(b, m).wait()
         mine_rows = pl.ds(0, m)
 
-        @pl.when(b == 0)
-        def _():
-            for n in range(1, DEEP - 1):
-                for t in a_copies(n, n):
-                    t.start(priority=BULK)
+        for n in range(1, DEEP - 1):
+            for t in a_copies(n, n):
+                t.start(priority=BULK)
 
         def a_step(n, clock):
             s, clock = lax.rem(n, DEEP), advance(clock, long_a)
@@ -299,9 +297,9 @@
             def _():
                 b_copy(par0, i + 1, 0).start(priority=BULK)
 
-            @pl.when((i >= 5 - DEEP) & (b + 1 < blocks))
-            def _():
-                for t in a_copies(i - (5 - DEEP), i - (5 - DEEP)):
+            @pl.when((i == 3) & (b + 1 < blocks))
+            def _():
+                for t in a_copies(0, 0):
                     t.start(priority=BULK)
 
             after(clock)
@@ -400,7 +398,7 @@
     dst, held, read, written = refs[-4:]
 
     def move(k):
-        rows = pl.ds((first + k) * CHUNK, CHUNK)
+        rows = pl.ds((first + k) * PIECE, PIECE)
         return (
             pltpu.make_async_copy(src.at[rows, :], held.at[k], read.at[k]),
             pltpu.make_async_copy(held.at[k], dst.at[rows, :], written.at[k]),
@@ -489,16 +487,16 @@
             out_shape=out,
             in_specs=[any_] * (1 + len(extra)),
             out_specs=any_,
-            scratch_shapes=[pltpu.VMEM((count, CHUNK, d), BF16), dma((count,)), dma((count,))],
+            scratch_shapes=[pltpu.VMEM((count, PIECE, d), BF16), dma((count,)), dma((count,))],
             input_output_aliases=alias,
             compiler_params=params,
-            cost_estimate=pl.CostEstimate(flops=count * COPY_FLOPS, bytes_accessed=count * CHUNK * d * 4, transcendentals=0),
+            cost_estimate=pl.CostEstimate(flops=count * COPY_FLOPS, bytes_accessed=count * PIECE * d * 4, transcendentals=0),
             name=name,
         )(summed, *extra)
 
     own, y = lax.optimization_barrier((own, copy_call(0, FIRST, (), {}, "copy_first")))
     par = lax.ppermute(own, "tp", [(0, 1), (1, 0), (6, 7), (7, 6)])
-    y = copy_call(FIRST, rows // CHUNK - FIRST, (own, y), {2: 0}, "copy_rest")
+    y = copy_call(FIRST, rows // PIECE - FIRST, (own, y), {2: 0}, "copy_rest")
     return pl.pallas_call(
         add_late,
         out_shape=out,

time: 468 us -> 465 us (level)
  no operation moved by 1% of the time
where the time goes in v4:
time: 465 us
  Pallas kernels  461 us (99%)
    pallas_call x1, Pallas kernels, block_call(): pl.pallas_call(kernel, out_shape=[jax.ShapeDtypeStruct((rows, d), BF16),...  435 us
    pallas_call x2, Pallas kernels, copy_call(): pl.pallas_call(functools.partial(copy_rows, first, count), out_shape=out,...  24.1 us
  transfers between devices with their start and end apart: 2, of which 0 were waited for; matrix products, arithmetic and copies ran while one was open for 0% of the time, Pallas kernels for 5%

profile of v4, /device:TPU:0, one launch (start us, length us, event | category | flops | bytes accessed | tf_op | source)
XLA Modules:
  0.0 464.9 jit_solution(1296666501221316295)
XLA Ops:
  0.0 435.2 %mlp_block.1 = (bf16[2048,8192]{1,0:T(8,128)(2,1)}, bf16[2048,4096]{1,0:T(8,128)(2,1)}, bf16[128,2048]{1,0:T(8,128)(2,1)}) custom-call(bf16[2048,8192]{1,0:T(8,128)(2,1)} %x.1, bf16[8192,3072]{1,0:T(8,128)(2,1)} %wg.1, bf16[8192,3072]{1,0:T(8,128)(2,1)} %wu.1, bf16[3072,8192]{1,0:T(8,128)(2,1)} %wd.1), custom_call_target="tpu_custom_call" | custom-call | flops 309237645312 | bytes 1000000000 | tf_op jit(solution)/shard_map/mlp_block/pallas_call | solution.py:448
  435.2 1.3 collective-permute-start
  436.5 16.1 %copy_first.1.refs_1_ = bf16[2048,8192]{1,0:T(8,128)(2,1)} custom-call(bf16[2048,8192]{1,0:T(8,128)(2,1)} %get-tuple-element.9.src), custom_call_target="tpu_custom_call" | custom-call | flops 11000000512 | bytes 46137344 | tf_op jit(solution)/shard_map/copy_first/pallas_call | solution.py:485
  452.6 0.0 collective-permute-done.refs_0_.own
  452.6 2.2 collective-permute-start.1
  454.8 8.0 %copy_rest.1.y_in = bf16[2048,8192]{1,0:T(8,128)(2,1)} custom-call(bf16[2048,8192]{1,0:T(8,128)(2,1)} %get-tuple-element.9.src, bf16[128,2048]{1,0:T(8,128)(2,1)} %collective-permute-done.refs_0_.own, bf16[2048,8192]{1,0:T(8,128)(2,1)} %copy_first.1.refs_1_), custom_call_target="tpu_custom_call", output_to_operand_aliasing={{}: (2, {})} | custom-call | flops 5000000000 | bytes 20971520 | tf_op jit(solution)/shard_map/copy_rest/pallas_call | solution.py:485
  462.9 0.0 collective-permute-done.1.par
  462.9 2.1 late_chunks.1
Async XLA Ops:
  435.2 17.4 %collective-permute-start = (bf16[128,2048]{1,0:T(8,128)(2,1)}, bf16[128,2048]{1,0:T(8,128)(2,1)}, u32[]{:S(2)}, u32[]{:S(2)}) collective-permute-start(bf16[128,2048]{1,0:T(8,128)(2,1)} %get-tuple-element.10), channel_id=1, source_target_pairs={{2,0},{3,1},{4,6},{5,7},{10,8},{11,9},{12,14},{13,15},{18,16},{19,... | collective-permute-start | bytes 1572872 | tf_op jit(solution)/shard_map/ppermute | solution.py:480
  452.6 10.3 %collective-permute-start.1 = (bf16[128,2048]{1,0:T(8,128)(2,1)}, bf16[128,2048]{1,0:T(8,128)(2,1)}, u32[]{:S(2)}, u32[]{:S(2)}) collective-permute-start(bf16[128,2048]{1,0:T(8,128)(2,1)} %collective-permute-done.refs_0_.own), channel_id=1, source_target_pairs={{0,1},{1,0},{6,7},{7,6},{8,9},{9,8},{14,15},{15,14},{16,17},{17,16... | collective-permute-start | bytes 1572872 | tf_op jit(solution)/shard_map/ppermute | solution.py:498

commit v5 on v4

--- a/solution.py
+++ b/solution.py
@@ -11,7 +11,7 @@
 BF16, F32 = jnp.bfloat16, jnp.float32
 BLOCK, CHUNK, NA = 384, 128, 256
 BULK = 1
-PIECE, FIRST, COPY_FLOPS = 32, 44, 25 * 10**7
+PIECE, FIRST, COPY_FLOPS = 16, 88, 125 * 10**6
 LATE = 2
 VMEM = 67043328
 SLOTS, RING, DEEP = 8, 4, 3

time: 465 us -> 466 us (level)
  no operation moved by 1% of the time
where the time goes in v5:
time: 466 us
  Pallas kernels  463 us (99%)
    pallas_call x1, Pallas kernels, block_call(): pl.pallas_call(kernel, out_shape=[jax.ShapeDtypeStruct((rows, d), BF16),...  435 us
    pallas_call x2, Pallas kernels, copy_call(): pl.pallas_call(functools.partial(copy_rows, first, count), out_shape=out,...  25.3 us
  transfers between devices with their start and end apart: 2, of which 0 were waited for; matrix products, arithmetic and copies ran while one was open for 0% of the time, Pallas kernels for 5%

profile of v5, /device:TPU:0, one launch (start us, length us, event | category | flops | bytes accessed | tf_op | source)
XLA Modules:
  0.0 466.1 jit_solution(5061944671156121969)
XLA Ops:
  0.0 435.2 %mlp_block.1 = (bf16[2048,8192]{1,0:T(8,128)(2,1)}, bf16[2048,4096]{1,0:T(8,128)(2,1)}, bf16[128,2048]{1,0:T(8,128)(2,1)}) custom-call(bf16[2048,8192]{1,0:T(8,128)(2,1)} %x.1, bf16[8192,3072]{1,0:T(8,128)(2,1)} %wg.1, bf16[8192,3072]{1,0:T(8,128)(2,1)} %wu.1, bf16[3072,8192]{1,0:T(8,128)(2,1)} %wd.1), custom_call_target="tpu_custom_call" | custom-call | flops 309237645312 | bytes 1000000000 | tf_op jit(solution)/shard_map/mlp_block/pallas_call | solution.py:448
  435.2 1.3 collective-permute-start
  436.5 17.1 %copy_first.1.refs_1_ = bf16[2048,8192]{1,0:T(8,128)(2,1)} custom-call(bf16[2048,8192]{1,0:T(8,128)(2,1)} %get-tuple-element.9.src), custom_call_target="tpu_custom_call" | custom-call | flops 11000000512 | bytes 46137344 | tf_op jit(solution)/shard_map/copy_first/pallas_call | solution.py:485
  453.5 0.0 collective-permute-done.refs_0_.own
  453.6 2.2 collective-permute-start.1
  455.8 8.3 %copy_rest.1.y_in = bf16[2048,8192]{1,0:T(8,128)(2,1)} custom-call(bf16[2048,8192]{1,0:T(8,128)(2,1)} %get-tuple-element.9.src, bf16[128,2048]{1,0:T(8,128)(2,1)} %collective-permute-done.refs_0_.own, bf16[2048,8192]{1,0:T(8,128)(2,1)} %copy_first.1.refs_1_), custom_call_target="tpu_custom_call", output_to_operand_aliasing={{}: (2, {})} | custom-call | flops 5000000000 | bytes 20971520 | tf_op jit(solution)/shard_map/copy_rest/pallas_call | solution.py:485
  464.1 0.0 collective-permute-done.1.par
  464.1 2.1 late_chunks.1
Async XLA Ops:
  435.2 18.4 %collective-permute-start = (bf16[128,2048]{1,0:T(8,128)(2,1)}, bf16[128,2048]{1,0:T(8,128)(2,1)}, u32[]{:S(2)}, u32[]{:S(2)}) collective-permute-start(bf16[128,2048]{1,0:T(8,128)(2,1)} %get-tuple-element.10), channel_id=1, source_target_pairs={{2,0},{3,1},{4,6},{5,7},{10,8},{11,9},{12,14},{13,15},{18,16},{19,... | collective-permute-start | bytes 1572872 | tf_op jit(solution)/shard_map/ppermute | solution.py:480
  453.6 10.5 %collective-permute-start.1 = (bf16[128,2048]{1,0:T(8,128)(2,1)}, bf16[128,2048]{1,0:T(8,128)(2,1)}, u32[]{:S(2)}, u32[]{:S(2)}) collective-permute-start(bf16[128,2048]{1,0:T(8,128)(2,1)} %collective-permute-done.refs_0_.own), channel_id=1, source_target_pairs={{0,1},{1,0},{6,7},{7,6},{8,9},{9,8},{14,15},{15,14},{16,17},{17,16... | collective-permute-start | bytes 1572872 | tf_op jit(solution)/shard_map/ppermute | solution.py:498
